TPU v7x, 32 devices: a whole 2x2x4 slice. The times are simulated.
32 devices in a mesh: prow: 2 (over x), pcol: 16 (over z, y, core).
Axes of the slice: x: 2, y: 2, z: 4, core: 2. Of those that a mesh axis runs over, the one named last changes fastest.
Arguments:
- vectors: float32 [32768, 2048], P('prow', 'pcol'), may hold values from -6 to 6
- reflectors: bfloat16 [4, 256, 32768], P(None, 'pcol', 'prow'), may hold values from -0.03125 to 0.03125
- tau_diag: float32 [4, 256], replicated, may hold values from 0.5 to 1.5
- coupling: float32 [4, 256, 256], replicated, may hold values from -0.375 to 0.375
Outputs:
- result: float32 [32768, 2048], P('prow', 'pcol')
All inputs are finite; a program needn't handle non-finite values.
Results may differ from a plain program's by a relative error of at most 0.0003.
Values may be sent and summed in bfloat16 or wider, within the bound.
A program may use at most 128 MiB of HBM per device.

v0:
```python
import jax
import jax.numpy as jnp
from jax import lax
from jax.sharding import PartitionSpec as P


def on_device(vectors, reflectors, tau_diag, coupling):
    count = reflectors.shape[0]
    gathered = lax.all_gather(reflectors, "pcol", axis=1, tiled=True)
    current = vectors
    for position in range(count - 1, -1, -1):
        rows_panel = gathered[position]
        widened = rows_panel.astype(jnp.float32)
        tri_factor = jnp.diag(tau_diag[position]) + jnp.triu(coupling[position], 1)
        partial_sum = jnp.dot(
            widened, current, precision=lax.Precision.HIGHEST, preferred_element_type=jnp.float32
        )
        totals = lax.psum(partial_sum, "prow")
        updates = jnp.dot(
            tri_factor, totals, precision=lax.Precision.HIGHEST, preferred_element_type=jnp.float32
        )
        current = current - lax.dot_general(
            widened,
            updates,
            (((0,), (0,)), ((), ())),
            precision=lax.Precision.HIGHEST,
            preferred_element_type=jnp.float32,
        )
    return current


def solution(mesh):
    return jax.shard_map(
        on_device,
        mesh=mesh,
        in_specs=(P("prow", "pcol"), P(None, "pcol", "prow"), P(), P()),
        out_specs=P("prow", "pcol"),
        check_vma=False,
    )
```

profile of v0, /device:TPU:0, one launch (start us, length us, event | category | flops | bytes accessed | tf_op | source)
XLA Modules:
  0.0 387.7 jit_solution(3231491931866824591)
XLA Ops:
  6.5 0.0 all-gather.2.cloned.1.call-start
  6.5 0.7 all-gather.2.cloned.1.call-update
  7.3 0.0 all-reduce.5.cloned.1.call-start
  7.3 9.0 %copy.5 = f32[16384,128]{0,1:T(8,128)} copy(f32[16384,128]{1,0:T(8,128)} %param.4) | data formatting | bytes 16777216 | tf_op args[0]
  16.3 0.0 copy-start.3
  16.3 0.0 copy-start.4
  16.3 163.4 %all-gather.2.cloned.1.call-done = bf16[4,256,16384]{2,1,0:T(8,128)(2,1)} async-done(((bf16[4,16,16384]{2,1,0:T(8,128)(2,1)}), bf16[4,256,16384]{2,1,0:T(8,128)(2,1)}) %all-gather.2.cloned.1.call-update) | async-done | bytes 33554448 | tf_op jit(solution)/shard_map/all_gather | solution.py:9
  179.7 11.2 %fusion.4 = f32[256,128]{1,0:T(8,128)} fusion(f32[16384,128]{1,0:T(8,128)} %param.4, bf16[4,256,16384]{2,1,0:T(8,128)(2,1)} %all-gather.2.cloned.1.call-done), kind=kOutput, calls=%fused_computation.12 | convolution fusion | flops 6442450944 | bytes 16908288 | tf_op jit(solution)/shard_map/dot_general | solution.py:15
  190.9 0.0 all-reduce.5.cloned.1.call-update
  190.9 0.2 all-reduce.7.cloned.1.call-start
  191.2 0.0 copy-done.3
  191.2 21.4 %all-reduce.5.cloned.1.call-done = f32[256,128]{1,0:T(8,128)} async-done(((f32[256,128]{1,0:T(8,128)}), f32[256,128]{1,0:T(8,128)}) %all-reduce.5.cloned.1.call-update) | async-done | bytes 131088 | tf_op jit(solution)/shard_map/psum | solution.py:18
  212.6 0.0 copy-done.4
  212.6 1.3 fusion.21
  213.9 9.4 %fusion.3 = f32[16384,128]{0,1:T(8,128)S(1)} fusion(f32[16384,128]{0,1:T(8,128)} %copy.5, f32[256,128]{1,0:T(8,128)S(1)} %fusion.21, bf16[4,256,16384]{2,1,0:T(8,128)(2,1)} %all-gather.2.cloned.1.call-done), kind=kOutput, calls=%fused_computation.7 | convolution fusion | flops 6444548096 | bytes 25296896 | tf_op jit(solution)/shard_map/dot_general | solution.py:22
  223.3 0.0 copy-start
  223.3 3.4 copy-done
  226.7 12.5 %fusion.10 = f32[256,128]{0,1:T(8,128)} fusion(f32[16384,128]{0,1:T(8,128)S(1)} %fusion.3, bf16[4,256,16384]{2,1,0:T(8,128)(2,1)} %all-gather.2.cloned.1.call-done), kind=kOutput, calls=%fused_computation.18 | convolution fusion | flops 6442450944 | bytes 16908288 | tf_op jit(solution)/shard_map/dot_general | solution.py:15
  239.2 0.0 all-reduce.7.cloned.1.call-update
  239.2 0.3 all-reduce.9.cloned.1.call-start
  239.5 21.4 %all-reduce.7.cloned.1.call-done = f32[256,128]{0,1:T(8,128)} async-done(((f32[256,128]{0,1:T(8,128)}), f32[256,128]{0,1:T(8,128)}) %all-reduce.7.cloned.1.call-update) | async-done | bytes 131088 | tf_op jit(solution)/shard_map/psum | solution.py:18
  260.9 1.3 fusion.18
  262.2 9.4 %fusion.2 = f32[16384,128]{0,1:T(8,128)S(1)} fusion(f32[16384,128]{0,1:T(8,128)} %copy-done, f32[256,128]{1,0:T(8,128)S(1)} %fusion.18, bf16[4,256,16384]{2,1,0:T(8,128)(2,1)} %all-gather.2.cloned.1.call-done), kind=kOutput, calls=%fused_computation.5 | convolution fusion | flops 6444548096 | bytes 25296896 | tf_op jit(solution)/shard_map/dot_general | solution.py:22
  271.6 0.0 copy-start.1
  271.6 3.4 copy-done.1
  275.0 12.5 %fusion.9 = f32[256,128]{0,1:T(8,128)} fusion(f32[16384,128]{0,1:T(8,128)S(1)} %fusion.2, bf16[4,256,16384]{2,1,0:T(8,128)(2,1)} %all-gather.2.cloned.1.call-done), kind=kOutput, calls=%fused_computation.17 | convolution fusion | flops 6442450944 | bytes 16908288 | tf_op jit(solution)/shard_map/dot_general | solution.py:15
  287.5 0.0 all-reduce.9.cloned.1.call-update
  287.5 0.3 all-reduce.11.cloned.1.call-start
  287.8 21.4 %all-reduce.9.cloned.1.call-done = f32[256,128]{0,1:T(8,128)} async-done(((f32[256,128]{0,1:T(8,128)}), f32[256,128]{0,1:T(8,128)}) %all-reduce.9.cloned.1.call-update) | async-done | bytes 131088 | tf_op jit(solution)/shard_map/psum | solution.py:18
  309.2 1.3 fusion.15
  310.5 9.4 %fusion.1 = f32[16384,128]{0,1:T(8,128)S(1)} fusion(f32[16384,128]{0,1:T(8,128)} %copy-done.1, f32[256,128]{1,0:T(8,128)S(1)} %fusion.15, bf16[4,256,16384]{2,1,0:T(8,128)(2,1)} %all-gather.2.cloned.1.call-done), kind=kOutput, calls=%fused_computation.3 | convolution fusion | flops 6444548096 | bytes 25296896 | tf_op jit(solution)/shard_map/dot_general | solution.py:22
  319.8 0.0 copy-start.2
  319.9 3.4 copy-done.2
  323.2 12.5 %fusion.8 = f32[256,128]{0,1:T(8,128)} fusion(f32[16384,128]{0,1:T(8,128)S(1)} %fusion.1, bf16[4,256,16384]{2,1,0:T(8,128)(2,1)} %all-gather.2.cloned.1.call-done), kind=kOutput, calls=%fused_computation.16 | convolution fusion | flops 6442450944 | bytes 16908288 | tf_op jit(solution)/shard_map/dot_general | solution.py:15
  335.7 0.0 all-reduce.11.cloned.1.call-update
  335.8 21.7 %all-reduce.11.cloned.1.call-done = f32[256,128]{0,1:T(8,128)} async-done(((f32[256,128]{0,1:T(8,128)}), f32[256,128]{0,1:T(8,128)}) %all-reduce.11.cloned.1.call-update) | async-done | bytes 131088 | tf_op jit(solution)/shard_map/psum | solution.py:18
  357.5 1.3 fusion.12
  358.8 12.9 %fusion = f32[16384,128]{0,1:T(8,128)} fusion(f32[16384,128]{0,1:T(8,128)} %copy-done.2, f32[256,128]{1,0:T(8,128)S(1)} %fusion.12, bf16[4,256,16384]{2,1,0:T(8,128)(2,1)} %all-gather.2.cloned.1.call-done), kind=kOutput, calls=%fused_computation.1 | convolution fusion | flops 6444548096 | bytes 25296896 | tf_op jit(solution)/shard_map/dot_general | solution.py:22
  371.7 9.0 %copy.6 = f32[16384,128]{1,0:T(8,128)} copy(f32[16384,128]{0,1:T(8,128)} %fusion) | data formatting | bytes 16777216 | tf_op jit(solution)/shard_map/sub | solution.py:22
  (1 shorter events, 0.0 us)
Async XLA Ops:
  6.5 173.1 %all-gather.2.cloned.1.call-start = ((), (), s32[]{:S(2)}) async-start(), calls=%async_computation | async-start | bytes 35651584 | tf_op jit(solution)/shard_map/all_gather | solution.py:9
  7.3 205.4 %all-reduce.5.cloned.1.call-start = ((), (), s32[]{:S(2)}) async-start(), calls=%async_computation.1 | async-start | bytes 262144 | tf_op jit(solution)/shard_map/psum | solution.py:18
  16.3 174.9 %copy-start.3 = (f32[4,256]{1,0:T(4,128)S(1)}, f32[4,256]{1,0:T(4,128)}, u32[]{:S(2)}) copy-start(f32[4,256]{1,0:T(4,128)} %param.6) | copy-start | bytes 12292
  16.3 196.3 %copy-start.4 = (f32[4,256,256]{2,1,0:T(8,128)S(1)}, f32[4,256,256]{2,1,0:T(8,128)}, u32[]{:S(2)}) copy-start(f32[4,256,256]{2,1,0:T(8,128)} %param.7) | copy-start | bytes 3145732
  190.9 70.0 %all-reduce.7.cloned.1.call-start = ((), (), s32[]{:S(2)}) async-start(), calls=%async_computation.2 | async-start | bytes 262144 | tf_op jit(solution)/shard_map/psum | solution.py:18
  223.3 3.4 copy-start
  239.2 70.0 %all-reduce.9.cloned.1.call-start = ((), (), s32[]{:S(2)}) async-start(), calls=%async_computation.3 | async-start | bytes 262144 | tf_op jit(solution)/shard_map/psum | solution.py:18
  271.6 3.4 copy-start.1
  287.5 70.0 %all-reduce.11.cloned.1.call-start = ((), (), s32[]{:S(2)}) async-start(), calls=%async_computation.4 | async-start | bytes 262144 | tf_op jit(solution)/shard_map/psum | solution.py:18
  319.8 3.4 copy-start.2
Sparse Core Ops, SparseCore 0:
  8.9 170.7 all-gather.1
  191.1 21.5 all-reduce.4
  239.3 21.5 all-reduce.6
  287.6 21.5 all-reduce.8
  335.9 21.5 all-reduce.10
where the time goes:
time: 392 us; the launch traced here: 388 us
  waiting for transfers between devices  250 us (64%)
  matrix products  94.9 us (24%)
  local copies, waits for them, and re-layouts  28.2 us (7%)
  between operations  13.7 us (3%)
    all_gather x1, waiting for transfers between devices, on_device(): gathered = lax.all_gather(reflectors, 'pcol', axis=1, tiled=True)  163 us
    psum x4, waiting for transfers between devices, on_device(): totals = lax.psum(partial_sum, 'prow')  85.9 us
    dot_general x4, matrix products, on_device(): jnp.dot(widened, current, precision=lax.Precision.HIGHEST, preferred_elem...  48.7 us
    dot_general x4, matrix products, on_device(): lax.dot_general(widened, updates, (((0,), (0,)), ((), ())), precision=lax...  41 us
    unnamed x11, local copies, waits for them, and re-layouts  19.2 us
    sub x1, local copies, waits for them, and re-layouts, on_device(): current - lax.dot_general(widened, updates, (((0,), (0,)), ((), ())), pre...  8.98 us
  transfers between devices with their start and end apart: 5, of which 5 were waited for; matrix products, arithmetic and copies ran while one was open for 2% of the time, Pallas kernels for 0%

commit v1 on v0

--- a/solution.py
+++ b/solution.py
@@ -1,10 +1,18 @@
+import functools
+
 import jax
 import jax.numpy as jnp
 from jax import lax
+from jax.experimental import pallas as pl
+from jax.experimental.pallas import tpu as pltpu
 from jax.sharding import PartitionSpec as P
 
-
-def on_device(vectors, reflectors, tau_diag, coupling):
+MESH = pl.DeviceIdType.MESH
+CORES = 2
+SIDES = 2
+
+
+def plain(vectors, reflectors, tau_diag, coupling):
     count = reflectors.shape[0]
     gathered = lax.all_gather(reflectors, "pcol", axis=1, tiled=True)
     current = vectors
@@ -29,9 +37,250 @@
     return current
 
 
+def split(x):
+    high = x.astype(jnp.bfloat16)
+    low = (x - high.astype(jnp.float32)).astype(jnp.bfloat16)
+    return jnp.concatenate([high, low], axis=1)
+
+
+def joined(x):
+    width = x.shape[1] // 2
+    return x[:, :width] + x[:, width:]
+
+
+def kernel(
+    length, z_hbm, v_hbm, tau_ref, coup_ref, out_hbm,
+    v, z, acc, yhl, wsend, wrecv,
+    in_sem, z_sem, out_sem, ring_send, ring_recv, mate_send, mate_recv, w_send, w_recv,
+):
+    count, own, rows = v_hbm.shape
+    cols = z.shape[1]
+    nb = v.shape[1]
+    half = rows // 2
+    deep = length // SIDES
+    prow = lax.axis_index("prow")
+    pcol = lax.axis_index("pcol")
+    core = pcol % CORES
+    chip = pcol // CORES
+    slow, side = chip // SIDES, chip % SIDES
+    place = slow * (1 - 2 * side) + (length - 1) * side
+
+    def pcol_at(position):
+        position = (position + length) % length
+        on = position // deep
+        deep_at = position * (1 - 2 * on) + (length - 1) * on
+        return (deep_at * SIDES + on) * CORES + core
+
+    ahead = [pcol_at(place + 1), pcol_at(place - 1)]
+    mate = chip * CORES + (1 - core)
+    across = 1 - prow
+
+    def shard(k, origin, lo, size):
+        start = pl.multiple_of(origin * own, own)
+        return v.at[count - 1 - k, pl.ds(start, own), pl.ds(lo, size)]
+
+    far = length // 2
+    last = 2 * (far - 1)
+
+    def ring(k, d, t):
+        hop = t // 2
+        origin = pcol_at(place - hop if d == 0 else place + hop)
+        h = d if t == last else t % 2
+        ref = shard(k, origin, h * half, half)
+        return pltpu.make_async_remote_copy(
+            src_ref=ref, dst_ref=ref, send_sem=ring_send.at[k, d, t], recv_sem=ring_recv.at[k, d, t],
+            device_id=(prow, ahead[d]), device_id_type=MESH,
+        )
+
+    def to_mate(k, j):
+        if j == 0:
+            origin = pcol
+        elif j < far:
+            origin = pcol_at(place - j)
+        elif j < 2 * far - 1:
+            origin = pcol_at(place + (j - far + 1))
+        else:
+            origin = pcol_at(place + far)
+        ref = shard(k, origin, 0, rows)
+        return pltpu.make_async_remote_copy(
+            src_ref=ref, dst_ref=ref, send_sem=mate_send.at[k, j], recv_sem=mate_recv.at[k, j],
+            device_id=(prow, mate), device_id_type=MESH,
+        )
+
+    def load(k):
+        return pltpu.make_async_copy(
+            v_hbm.at[count - 1 - k], shard(k, pcol, 0, rows), in_sem.at[k]
+        )
+
+    z_in = pltpu.make_async_copy(z_hbm, z, z_sem)
+    for k in range(count):
+        load(k).start()
+    z_in.start()
+
+    barrier = pltpu.get_barrier_semaphore()
+    for target in ((prow, ahead[0]), (prow, ahead[1]), (prow, mate), (across, pcol)):
+        pl.semaphore_signal(barrier, inc=1, device_id=target, device_id_type=MESH)
+    pl.semaphore_wait(barrier, 4)
+
+    def begin(k):
+        load(k).wait()
+        for t in range(2):
+            for d in range(2):
+                ring(k, d, t).start()
+        to_mate(k, 0).start()
+
+    def arrived(k, t):
+        for d in range(2):
+            ring(k, d, t).wait_recv()
+            if t + 2 < last or (t + 2 == last and d == 0) or (t + 1 == last and d == 1):
+                ring(k, d, min(t + 2, last)).start()
+            if t % 2 == 1:
+                to_mate(k, (t + 1) // 2 + (far - 1) * d).start()
+        if t == last:
+            to_mate(k, 2 * far - 1).start()
+        if t == last - 1 and k + 1 < count:
+            begin(k + 1)
+
+    tile = min(1024, half)
+    tiles = rows // tile
+
+    def project(k, lo, hi):
+        @pl.loop(lo, hi)
+        def _(i):
+            at = pl.ds(pl.multiple_of(i * tile, tile), tile)
+            acc[...] += jnp.dot(
+                v[count - 1 - k, :, at], split(z[at, :]), preferred_element_type=jnp.float32
+            )
+
+    def to_across(k):
+        return pltpu.make_async_remote_copy(
+            src_ref=wsend.at[k], dst_ref=wrecv.at[k], send_sem=w_send.at[k], recv_sem=w_recv.at[k],
+            device_id=(across, pcol), device_id_type=MESH,
+        )
+
+    def factor(k):
+        p = count - 1 - k
+        row = lax.broadcasted_iota(jnp.int32, (nb, nb), 0)
+        col = lax.broadcasted_iota(jnp.int32, (nb, nb), 1)
+        upper = jnp.where(col > row, coup_ref[p], 0.0)
+        tri = jnp.where(col == row, tau_ref[p][None, :], upper)
+        totals = wsend[k] + wrecv[k]
+        y = jnp.dot(tri, totals, precision=lax.Precision.HIGHEST, preferred_element_type=jnp.float32)
+        yhl[...] = split(y)
+
+    def out_copy(i):
+        at = pl.ds(pl.multiple_of(i * tile, tile), tile)
+        return pltpu.make_async_copy(z.at[at, :], out_hbm.at[at, :], out_sem.at[i])
+
+    def update(k, lo, hi):
+        @pl.loop(lo, hi)
+        def _(i):
+            at = pl.ds(pl.multiple_of(i * tile, tile), tile)
+            change = lax.dot_general(
+                v[count - 1 - k, :, at], yhl[...], (((0,), (0,)), ((), ())),
+                preferred_element_type=jnp.float32,
+            )
+            z[at, :] = z[at, :] - joined(change)
+            if k == count - 1:
+                out_copy(i).start()
+
+    def compute(k):
+        def first():
+            for j in range(2 * far):
+                to_mate(k, j).wait_recv()
+            acc[...] = jnp.zeros_like(acc)
+            project(k, 0, tiles // 2)
+
+        def second():
+            project(k, tiles // 2, tiles)
+            wsend[k] = joined(acc[...])
+            to_across(k).start()
+
+        def third():
+            to_across(k).wait_recv()
+            factor(k)
+
+        quarter = tiles // 4
+        return [first, second, third] + [
+            functools.partial(update, k, q * quarter, (q + 1) * quarter) for q in range(4)
+        ]
+
+    begin(0)
+    for k in range(count):
+        work = compute(k - 1) if k else [z_in.wait]
+        for t in range(last + 1):
+            arrived(k, t)
+            if t < len(work):
+                work[t]()
+        for piece in work[last + 1:]:
+            piece()
+    for piece in compute(count - 1):
+        piece()
+    for k in range(count):
+        for d in range(2):
+            for t in range(last + 1):
+                ring(k, d, t).wait_send()
+        for j in range(2 * far):
+            to_mate(k, j).wait_send()
+        to_across(k).wait_send()
+    for i in range(tiles):
+        out_copy(i).wait()
+
+
+def fused(length, vectors, reflectors, tau_diag, coupling):
+    count, own, rows = reflectors.shape
+    cols = vectors.shape[1]
+    nb = own * length * CORES
+    tiles = rows // min(1024, rows // 2)
+    messages = length - 1
+    vmem = pl.BlockSpec(memory_space=pltpu.VMEM)
+    hbm = pl.BlockSpec(memory_space=pl.ANY)
+    dma = pltpu.SemaphoreType.DMA
+    return pl.pallas_call(
+        functools.partial(kernel, length),
+        out_shape=jax.ShapeDtypeStruct(vectors.shape, vectors.dtype),
+        in_specs=[hbm, hbm, vmem, vmem],
+        out_specs=hbm,
+        scratch_shapes=[
+            pltpu.VMEM((count, nb, rows), reflectors.dtype),
+            pltpu.VMEM((rows, cols), jnp.float32),
+            pltpu.VMEM((nb, 2 * cols), jnp.float32),
+            pltpu.VMEM((nb, 2 * cols), jnp.bfloat16),
+            pltpu.VMEM((count, nb, cols), jnp.float32),
+            pltpu.VMEM((count, nb, cols), jnp.float32),
+            dma((count,)),
+            dma,
+            dma((tiles,)),
+            dma((count, 2, messages)),
+            dma((count, 2, messages)),
+            dma((count, length)),
+            dma((count, length)),
+            dma((count,)),
+            dma((count,)),
+        ],
+        compiler_params=pltpu.CompilerParams(
+            collective_id=0, has_side_effects=True, vmem_limit_bytes=60 * 1024 * 1024
+        ),
+    )(vectors, reflectors, tau_diag, coupling)
+
+
+def on_device(two_rows, length, vectors, reflectors, tau_diag, coupling):
+    count, own, rows = reflectors.shape
+    cols = vectors.shape[1]
+    held = count * own * length * CORES * rows * 2 + rows * cols * 4
+    fits = (
+        two_rows and length % (2 * SIDES) == 0 and own % 16 == 0 and rows % 4096 == 0
+        and cols % 128 == 0 and held <= 48 * 1024 * 1024
+    )
+    if fits:
+        return fused(length, vectors, reflectors, tau_diag, coupling)
+    return plain(vectors, reflectors, tau_diag, coupling)
+
+
 def solution(mesh):
+    length = mesh.shape["pcol"] // CORES
     return jax.shard_map(
-        on_device,
+        functools.partial(on_device, mesh.shape["prow"] == 2, length),
         mesh=mesh,
         in_specs=(P("prow", "pcol"), P(None, "pcol", "prow"), P(), P()),
         out_specs=P("prow", "pcol"),

time: 392 us -> 196 us (0.50); the launches traced: 388 us -> 196 us
  waiting for transfers between devices: 250 us -> 0 us
  Pallas kernels: 0 us -> 190 us
  matrix products: 94.9 us -> 0 us
  local copies, waits for them, and re-layouts: 28.2 us -> 5.86 us
  between operations: 13.7 us -> 0.01 us
    pallas_call x0 -> x1, Pallas kernels: none -> 190 us  [fused(): pl.pallas_call(functools.partial(kernel, length), out_shape=jax.ShapeDtyp...]
    all_gather x1 -> x0, waiting for transfers between devices: 163 us -> none  [on_device(): gathered = lax.all_gather(reflectors, 'pcol', axis=1, tiled=True)]
    dot_general x12 -> x0, matrix products: 94.9 us -> none  [the longest x4 48.7 us: on_device(): jnp.dot(widened, current, precision=lax.Precision.HIGHEST, preferred_elem...]
    psum x4 -> x0, waiting for transfers between devices: 85.9 us -> none  [on_device(): totals = lax.psum(partial_sum, 'prow')]
    unnamed x11 -> x1, local copies, waits for them, and re-layouts: 19.2 us -> 5.86 us
    sub x1 -> x0, local copies, waits for them, and re-layouts: 8.98 us -> none  [on_device(): current - lax.dot_general(widened, updates, (((0,), (0,)), ((), ())), pre...]
  transfers between devices with their start and end apart: 5 -> 0, of which waited for: 5 -> 0; matrix products, arithmetic and copies ran while one was open for 2% -> 0% of each run, Pallas kernels for 0% -> 0%
where the time goes in v1:
time: 196 us
  Pallas kernels  190 us (97%)
  local copies, waits for them, and re-layouts  5.86 us (3%)
    pallas_call x1, Pallas kernels, fused(): pl.pallas_call(functools.partial(kernel, length), out_shape=jax.ShapeDtyp...  190 us
    unnamed x1, local copies, waits for them, and re-layouts  5.86 us

profile of v1, /device:TPU:0, one launch (start us, length us, event | category | flops | bytes accessed | tf_op | source)
XLA Modules:
  0.0 196.2 jit_solution(8712498953057952216)
XLA Ops:
  0.0 190.3 %shard_map.46 = f32[16384,128]{1,0:T(8,128)} custom-call(f32[16384,128]{1,0:T(8,128)} %z_hbm.1, bf16[4,16,16384]{2,1,0:T(8,128)(2,1)} %v_hbm.1, f32[4,256]{1,0:T(4,128)} %tau_ref.1, f32[4,256,256]{2,1,0:T(8,128)} %coup_ref.1), custom_call_target="tpu_custom_call" | custom-call | tf_op jit(solution)/shard_map/pallas_call | solution.py:239
  190.3 5.9 %copy.6 = f32[16384,128]{1,0:T(8,128)} copy(f32[16384,128]{1,0:T(8,128)} %shard_map.46) | data formatting | bytes 16777216

commit v2 on v1

v2 whole, which is shorter than its diff:
```python
import functools

import jax
import jax.numpy as jnp
from jax import lax
from jax.experimental import pallas as pl
from jax.experimental.pallas import tpu as pltpu
from jax.sharding import PartitionSpec as P

MESH = pl.DeviceIdType.MESH
CORES = 2
SIDES = 2


def plain(vectors, reflectors, tau_diag, coupling):
    count = reflectors.shape[0]
    gathered = lax.all_gather(reflectors, "pcol", axis=1, tiled=True)
    current = vectors
    for position in range(count - 1, -1, -1):
        rows_panel = gathered[position]
        widened = rows_panel.astype(jnp.float32)
        tri_factor = jnp.diag(tau_diag[position]) + jnp.triu(coupling[position], 1)
        partial_sum = jnp.dot(
            widened, current, precision=lax.Precision.HIGHEST, preferred_element_type=jnp.float32
        )
        totals = lax.psum(partial_sum, "prow")
        updates = jnp.dot(
            tri_factor, totals, precision=lax.Precision.HIGHEST, preferred_element_type=jnp.float32
        )
        current = current - lax.dot_general(
            widened,
            updates,
            (((0,), (0,)), ((), ())),
            precision=lax.Precision.HIGHEST,
            preferred_element_type=jnp.float32,
        )
    return current


def split(x):
    high = x.astype(jnp.bfloat16)
    low = (x - high.astype(jnp.float32)).astype(jnp.bfloat16)
    return jnp.concatenate([high, low], axis=1)


def joined(x):
    width = x.shape[1] // 2
    return x[:, :width] + x[:, width:]


def kernel(
    length, z_hbm, v_hbm, tau_hbm, coup_hbm, out_hbm,
    v, z, zhl, acc, tau, tri, nat, yhl, wsend, wrecv,
    in_sem, z_sem, t_sem, out_sem, ring_send, ring_recv, mate_send, mate_recv, w_send, w_recv,
):
    count, own, rows = v_hbm.shape
    nb = v.shape[1]
    group = own * CORES
    half = rows // 2
    deep = length // SIDES
    final = count - 1
    prow = lax.axis_index("prow")
    pcol = lax.axis_index("pcol")
    core = pcol % CORES
    chip = pcol // CORES
    slow, side = chip // SIDES, chip % SIDES
    place = slow * (1 - 2 * side) + (length - 1) * side

    def chip_at(position):
        position = (position + length) % length
        on = position // deep
        return (position * (1 - 2 * on) + (length - 1) * on) * SIDES + on

    ahead = [chip_at(place + 1) * CORES + core, chip_at(place - 1) * CORES + core]
    mate = chip * CORES + (1 - core)
    across = 1 - prow
    far = length // 2
    last = 2 * (far - 1)

    def slot(d, hops):
        return 0 if hops == 0 else min(2 * hops - 1 + d, length - 1)

    def slot_chip(j):
        hops = (j + 1) // 2
        return chip_at(place - hops if j % 2 else place + hops)

    def shard(k, j, lo, size):
        start = pl.multiple_of((j * CORES + core) * own, own)
        return v.at[final - k, pl.ds(start, own), pl.ds(lo, size)]

    def ring(k, d, t):
        hops = t // 2
        h = d if t == last else (t + d) % 2
        return pltpu.make_async_remote_copy(
            src_ref=shard(k, slot(d, hops), h * half, half),
            dst_ref=shard(k, slot(d, hops + 1), h * half, half),
            send_sem=ring_send.at[k, d, t], recv_sem=ring_recv.at[k, d, t],
            device_id=(prow, ahead[d]), device_id_type=MESH,
        )

    def to_mate(k, j):
        ref = shard(k, j, 0, rows)
        return pltpu.make_async_remote_copy(
            src_ref=ref, dst_ref=ref, send_sem=mate_send.at[k, j], recv_sem=mate_recv.at[k, j],
            device_id=(prow, mate), device_id_type=MESH,
        )

    def load(k):
        return pltpu.make_async_copy(v_hbm.at[final - k], shard(k, 0, 0, rows), in_sem.at[k])

    load(0).start()
    barrier = pltpu.get_barrier_semaphore()
    for target in ((prow, ahead[0]), (prow, ahead[1]), (prow, mate), (across, pcol)):
        pl.semaphore_signal(barrier, inc=1, device_id=target, device_id_type=MESH)
    pl.semaphore_wait(barrier, 4)

    def begin(k):
        load(k).wait()
        for t in range(2):
            for d in range(2):
                ring(k, d, t).start()
        to_mate(k, 0).start()

    def arrived(k, t):
        for d in range(2):
            ring(k, d, t).wait_recv()
            if t + 2 <= last:
                ring(k, d, t + 2).start()
            if t % 2 == 1:
                to_mate(k, slot(d, (t + 1) // 2)).start()
        if t == last:
            to_mate(k, length - 1).start()
        if t == last - 2 and k < final:
            begin(k + 1)

    tile = min(1024, half)
    tiles = rows // tile

    def tile_at(i):
        return pl.ds(pl.multiple_of(i * tile, tile), tile)

    def project(k, lo, hi, first=0, beyond=nb):
        @pl.loop(lo, hi)
        def _(i):
            at = tile_at(i)
            acc[first:beyond, :] += jnp.dot(
                v[final - k, first:beyond, at], zhl[at, :], preferred_element_type=jnp.float32
            )

    cuts = [0, (length - 3) * group, (length - 1) * group, nb]

    def to_across(k, part=None):
        sem = k if part is None else final + part
        at = pl.ds(0, nb) if part is None else pl.ds(cuts[part], cuts[part + 1] - cuts[part])
        return pltpu.make_async_remote_copy(
            src_ref=wsend.at[k, at], dst_ref=wrecv.at[k, at], send_sem=w_send.at[sem], recv_sem=w_recv.at[sem],
            device_id=(across, pcol), device_id_type=MESH,
        )

    def mates(k, lo, hi):
        for j in range(lo, hi):
            to_mate(k, j).wait_recv()

    def factor(k):
        for j in range(length):
            mine = pl.ds(j * group, group)
            at = pl.ds(pl.multiple_of(slot_chip(j) * group, group), group)
            nat[at, :] = wsend[k, mine, :] + wrecv[k, mine, :]
        nat[...] = jnp.dot(
            tri[final - k], nat[...], precision=lax.Precision.HIGHEST, preferred_element_type=jnp.float32
        )
        for j in range(length):
            at = pl.ds(pl.multiple_of(slot_chip(j) * group, group), group)
            yhl[j * group:(j + 1) * group, :] = split(nat[at, :])

    def out_copy(i):
        at = tile_at(i)
        return pltpu.make_async_copy(z.at[at, :], out_hbm.at[at, :], out_sem.at[i])

    def update(k, lo, hi):
        @pl.loop(lo, hi)
        def _(i):
            at = tile_at(i)
            change = lax.dot_general(
                v[final - k, :, at], yhl[...], (((0,), (0,)), ((), ())),
                preferred_element_type=jnp.float32,
            )
            fresh = z[at, :] - joined(change)
            z[at, :] = fresh
            if k < final:
                zhl[at, :] = split(fresh)
            else:
                out_copy(i).start()

    def clear():
        acc[...] = jnp.zeros_like(acc)

    def head(k):
        mates(k, 0, length)
        clear()
        project(k, 0, tiles // 2)

    def rest(k):
        project(k, tiles // 2, tiles)
        wsend[k] = joined(acc[...])
        to_across(k).start()

    def solve(k):
        to_across(k).wait_recv()
        factor(k)

    def quarters(k):
        return [
            functools.partial(update, k, q * tiles // 4, (q + 1) * tiles // 4) for q in range(4)
        ]

    def finish(part):
        slots = [cuts[part] // group, cuts[part + 1] // group]
        mates(final, *slots)
        project(final, 0, tiles, cuts[part], cuts[part + 1])
        wsend[final, cuts[part]:cuts[part + 1], :] = joined(acc[cuts[part]:cuts[part + 1], :])
        to_across(final, part).start()

    def opening():
        z_in.wait()
        tau_in.wait()
        coup_in.wait()

        @pl.loop(0, tiles)
        def _(i):
            at = tile_at(i)
            zhl[at, :] = split(z[at, :])

    def triangles():
        row = lax.broadcasted_iota(jnp.int32, (nb, nb), 0)
        col = lax.broadcasted_iota(jnp.int32, (nb, nb), 1)
        for p in range(count):
            upper = jnp.where(col > row, tri[p], 0.0)
            tri[p] = jnp.where(col == row, tau[p][None, :], upper)

    begin(0)
    z_in = pltpu.make_async_copy(z_hbm, z, z_sem)
    tau_in = pltpu.make_async_copy(tau_hbm, tau, t_sem.at[0])
    coup_in = pltpu.make_async_copy(coup_hbm, tri, t_sem.at[1])
    for k in range(1, count):
        load(k).start()
    z_in.start()
    tau_in.start()
    coup_in.start()
    for k in range(count):
        if k == 0:
            work = [[opening], [triangles]]
        else:
            q = quarters(k - 1)
            a, b, c = [functools.partial(f, k - 1) for f in (head, rest, solve)]
            work = [[a], [b], [c]] + [[piece] for piece in q]
            if k == final:
                work = [[a], [b], [c, q[0]], [q[1], q[2]], [q[3], clear, functools.partial(finish, 0)]]
                work.append([functools.partial(finish, 1)])
        for t in range(last + 1):
            arrived(k, t)
            for piece in work[t] if t < len(work) else []:
                piece()
        for pieces in work[last + 1:]:
            for piece in pieces:
                piece()
    finish(2)
    for part in range(3):
        to_across(final, part).wait_recv()
    factor(final)
    update(final, 0, tiles)
    for k in range(count):
        for d in range(2):
            for t in range(last + 1):
                ring(k, d, t).wait_send()
        for j in range(length):
            to_mate(k, j).wait_send()
        if k < final:
            to_across(k).wait_send()
    for part in range(3):
        to_across(final, part).wait_send()
    for i in range(tiles):
        out_copy(i).wait()


def fused(length, vectors, reflectors, tau_diag, coupling):
    count, own, rows = reflectors.shape
    cols = vectors.shape[1]
    nb = own * length * CORES
    tiles = rows // min(1024, rows // 2)
    messages = length - 1
    hbm = pl.BlockSpec(memory_space=pl.ANY)
    dma = pltpu.SemaphoreType.DMA
    return pl.pallas_call(
        functools.partial(kernel, length),
        out_shape=jax.ShapeDtypeStruct(vectors.shape, vectors.dtype),
        in_specs=[hbm] * 4,
        out_specs=hbm,
        scratch_shapes=[
            pltpu.VMEM((count, nb, rows), reflectors.dtype),
            pltpu.VMEM((rows, cols), jnp.float32),
            pltpu.VMEM((rows, 2 * cols), jnp.bfloat16),
            pltpu.VMEM((nb, 2 * cols), jnp.float32),
            pltpu.VMEM((count, nb), jnp.float32),
            pltpu.VMEM((count, nb, nb), jnp.float32),
            pltpu.VMEM((nb, cols), jnp.float32),
            pltpu.VMEM((nb, 2 * cols), jnp.bfloat16),
            pltpu.VMEM((count, nb, cols), jnp.float32),
            pltpu.VMEM((count, nb, cols), jnp.float32),
            dma((count,)),
            dma,
            dma((2,)),
            dma((tiles,)),
            dma((count, 2, messages)),
            dma((count, 2, messages)),
            dma((count, length)),
            dma((count, length)),
            dma((count + 2,)),
            dma((count + 2,)),
        ],
        compiler_params=pltpu.CompilerParams(
            collective_id=0, has_side_effects=True, vmem_limit_bytes=60 * 1024 * 1024
        ),
    )(vectors, reflectors, tau_diag, coupling)


def on_device(two_rows, length, vectors, reflectors, tau_diag, coupling):
    count, own, rows = reflectors.shape
    cols = vectors.shape[1]
    held = count * own * length * CORES * rows * 2 + rows * cols * 8
    fits = (
        two_rows and length % (2 * SIDES) == 0 and length >= 8 and count >= 2 and own % 16 == 0 and rows % 4096 == 0
        and cols % 128 == 0 and held <= 52 * 1024 * 1024
    )
    if fits:
        return fused(length, vectors, reflectors, tau_diag, coupling)
    return plain(vectors, reflectors, tau_diag, coupling)


def solution(mesh):
    length = mesh.shape["pcol"] // CORES
    return jax.shard_map(
        functools.partial(on_device, mesh.shape["prow"] == 2, length),
        mesh=mesh,
        in_specs=(P("prow", "pcol"), P(None, "pcol", "prow"), P(), P()),
        out_specs=P("prow", "pcol"),
        check_vma=False,
    )
```

time: 196 us -> 187 us (0.954)
  Pallas kernels: 190 us -> 181 us
    pallas_call x1, Pallas kernels: 190 us -> 181 us  [fused(): pl.pallas_call(functools.partial(kernel, length), out_shape=jax.ShapeDtyp...]
where the time goes in v2:
time: 187 us; the launch traced here: 186 us
  Pallas kernels  181 us (97%)
  local copies, waits for them, and re-layouts  5.86 us (3%)
    pallas_call x1, Pallas kernels, fused(): pl.pallas_call(functools.partial(kernel, length), out_shape=jax.ShapeDtyp...  181 us
    unnamed x1, local copies, waits for them, and re-layouts  5.86 us

profile of v2, /device:TPU:0, one launch (start us, length us, event | category | flops | bytes accessed | tf_op | source)
XLA Modules:
  0.0 186.4 jit_solution(17162549433547758822)
XLA Ops:
  0.0 180.6 %shard_map.46 = f32[16384,128]{1,0:T(8,128)} custom-call(f32[16384,128]{1,0:T(8,128)} %z_hbm.1, bf16[4,16,16384]{2,1,0:T(8,128)(2,1)} %v_hbm.1, f32[4,256]{1,0:T(4,128)} %tau_hbm.1, f32[4,256,256]{2,1,0:T(8,128)} %coup_hbm.1), custom_call_target="tpu_custom_call" | custom-call | tf_op jit(solution)/shard_map/pallas_call | solution.py:294
  180.6 5.9 %copy.6 = f32[16384,128]{1,0:T(8,128)} copy(f32[16384,128]{1,0:T(8,128)} %shard_map.46) | data formatting | bytes 16777216

commit v3 on v2

--- a/solution.py
+++ b/solution.py
@@ -49,9 +49,9 @@
 
 
 def kernel(
-    length, z_hbm, v_hbm, tau_hbm, coup_hbm, out_hbm,
-    v, z, zhl, acc, tau, tri, nat, yhl, wsend, wrecv,
-    in_sem, z_sem, t_sem, out_sem, ring_send, ring_recv, mate_send, mate_recv, w_send, w_recv,
+    length, z_hbm, v_hbm, tau_hbm, coup_hbm, z,
+    v, zhl, acc, tau, tri, nat, yhl, wsend, wrecv,
+    in_sem, z_sem, t_sem, ring_send, ring_recv, mate_send, mate_recv, w_send, w_recv,
 ):
     count, own, rows = v_hbm.shape
     nb = v.shape[1]
@@ -173,10 +173,6 @@
             at = pl.ds(pl.multiple_of(slot_chip(j) * group, group), group)
             yhl[j * group:(j + 1) * group, :] = split(nat[at, :])
 
-    def out_copy(i):
-        at = tile_at(i)
-        return pltpu.make_async_copy(z.at[at, :], out_hbm.at[at, :], out_sem.at[i])
-
     def update(k, lo, hi):
         @pl.loop(lo, hi)
         def _(i):
@@ -189,8 +185,6 @@
             z[at, :] = fresh
             if k < final:
                 zhl[at, :] = split(fresh)
-            else:
-                out_copy(i).start()
 
     def clear():
         acc[...] = jnp.zeros_like(acc)
@@ -279,26 +273,22 @@
             to_across(k).wait_send()
     for part in range(3):
         to_across(final, part).wait_send()
-    for i in range(tiles):
-        out_copy(i).wait()
 
 
 def fused(length, vectors, reflectors, tau_diag, coupling):
     count, own, rows = reflectors.shape
     cols = vectors.shape[1]
     nb = own * length * CORES
-    tiles = rows // min(1024, rows // 2)
     messages = length - 1
     hbm = pl.BlockSpec(memory_space=pl.ANY)
     dma = pltpu.SemaphoreType.DMA
     return pl.pallas_call(
         functools.partial(kernel, length),
-        out_shape=jax.ShapeDtypeStruct(vectors.shape, vectors.dtype),
+        out_shape=pltpu.VMEM(vectors.shape, vectors.dtype),
         in_specs=[hbm] * 4,
-        out_specs=hbm,
+        out_specs=pl.BlockSpec(memory_space=pltpu.VMEM),
         scratch_shapes=[
             pltpu.VMEM((count, nb, rows), reflectors.dtype),
-            pltpu.VMEM((rows, cols), jnp.float32),
             pltpu.VMEM((rows, 2 * cols), jnp.bfloat16),
             pltpu.VMEM((nb, 2 * cols), jnp.float32),
             pltpu.VMEM((count, nb), jnp.float32),
@@ -310,7 +300,6 @@
             dma((count,)),
             dma,
             dma((2,)),
-            dma((tiles,)),
             dma((count, 2, messages)),
             dma((count, 2, messages)),
             dma((count, length)),
@@ -319,7 +308,7 @@
             dma((count + 2,)),
         ],
         compiler_params=pltpu.CompilerParams(
-            collective_id=0, has_side_effects=True, vmem_limit_bytes=60 * 1024 * 1024
+            collective_id=0, has_side_effects=True, vmem_limit_bytes=48 * 1024 * 1024
         ),
     )(vectors, reflectors, tau_diag, coupling)
 

time: 187 us -> 183 us (0.979)
  local copies, waits for them, and re-layouts: 5.86 us -> 3.4 us
    unnamed x1, local copies, waits for them, and re-layouts: 5.86 us -> 3.4 us
where the time goes in v3:
time: 183 us
  Pallas kernels  180 us (98%)
  local copies, waits for them, and re-layouts  3.4 us (2%)
    pallas_call x1, Pallas kernels, fused(): pl.pallas_call(functools.partial(kernel, length), out_shape=pltpu.VMEM(ve...  180 us

profile of v3, /device:TPU:0, one launch (start us, length us, event | category | flops | bytes accessed | tf_op | source)
XLA Modules:
  0.0 183.2 jit_solution(9326309946247888179)
XLA Ops:
  0.0 179.8 %shard_map.46 = f32[16384,128]{1,0:T(8,128)S(1)} custom-call(f32[16384,128]{1,0:T(8,128)} %z_hbm.1, bf16[4,16,16384]{2,1,0:T(8,128)(2,1)} %v_hbm.1, f32[4,256]{1,0:T(4,128)} %tau_hbm.1, f32[4,256,256]{2,1,0:T(8,128)} %coup_hbm.1), custom_call_target="tpu_custom_call" | custom-call | tf_op jit(solution)/shard_map/pallas_call | solution.py:285
  179.8 3.4 %copy.6 = f32[16384,128]{1,0:T(8,128)} copy(f32[16384,128]{1,0:T(8,128)S(1)} %shard_map.46) | data formatting | bytes 16777216

commit v4 on v3

--- a/solution.py
+++ b/solution.py
@@ -49,12 +49,12 @@
 
 
 def kernel(
-    length, z_hbm, v_hbm, tau_hbm, coup_hbm, z,
-    v, zhl, acc, tau, tri, nat, yhl, wsend, wrecv,
+    length, z_hbm, v_hbm, tau_hbm, coup_hbm, z, ending, yhl,
+    v, zhl, acc, tau, tri, nat, wsend, wrecv,
     in_sem, z_sem, t_sem, ring_send, ring_recv, mate_send, mate_recv, w_send, w_recv,
 ):
     count, own, rows = v_hbm.shape
-    nb = v.shape[1]
+    nb = ending.shape[0]
     group = own * CORES
     half = rows // 2
     deep = length // SIDES
@@ -86,7 +86,8 @@
 
     def shard(k, j, lo, size):
         start = pl.multiple_of((j * CORES + core) * own, own)
-        return v.at[final - k, pl.ds(start, own), pl.ds(lo, size)]
+        at = (pl.ds(start, own), pl.ds(lo, size))
+        return ending.at[at] if k == final else v.at[(k,) + at]
 
     def ring(k, d, t):
         hops = t // 2
@@ -139,12 +140,15 @@
     def tile_at(i):
         return pl.ds(pl.multiple_of(i * tile, tile), tile)
 
+    def panel(k):
+        return ending if k == final else v.at[k]
+
     def project(k, lo, hi, first=0, beyond=nb):
         @pl.loop(lo, hi)
         def _(i):
             at = tile_at(i)
             acc[first:beyond, :] += jnp.dot(
-                v[final - k, first:beyond, at], zhl[at, :], preferred_element_type=jnp.float32
+                panel(k)[first:beyond, at], zhl[at, :], preferred_element_type=jnp.float32
             )
 
     cuts = [0, (length - 3) * group, (length - 1) * group, nb]
@@ -178,13 +182,12 @@
         def _(i):
             at = tile_at(i)
             change = lax.dot_general(
-                v[final - k, :, at], yhl[...], (((0,), (0,)), ((), ())),
+                panel(k)[:, at], yhl[...], (((0,), (0,)), ((), ())),
                 preferred_element_type=jnp.float32,
             )
             fresh = z[at, :] - joined(change)
             z[at, :] = fresh
-            if k < final:
-                zhl[at, :] = split(fresh)
+            zhl[at, :] = split(fresh)
 
     def clear():
         acc[...] = jnp.zeros_like(acc)
@@ -262,7 +265,6 @@
     for part in range(3):
         to_across(final, part).wait_recv()
     factor(final)
-    update(final, 0, tiles)
     for k in range(count):
         for d in range(2):
             for t in range(last + 1):
@@ -275,26 +277,52 @@
         to_across(final, part).wait_send()
 
 
+def closing(z, panel, yhl, out_hbm, fresh, out_sem):
+    tiles = out_sem.shape[0]
+    tile = z.shape[0] // tiles
+
+    def out_copy(i):
+        at = pl.ds(pl.multiple_of(i * tile, tile), tile)
+        return pltpu.make_async_copy(fresh.at[at, :], out_hbm.at[at, :], out_sem.at[i])
+
+    @pl.loop(0, tiles)
+    def _(i):
+        at = pl.ds(pl.multiple_of(i * tile, tile), tile)
+        change = lax.dot_general(
+            panel[:, at], yhl[...], (((0,), (0,)), ((), ())), preferred_element_type=jnp.float32
+        )
+        fresh[at, :] = z[at, :] - joined(change)
+        out_copy(i).start()
+
+    @pl.loop(0, tiles)
+    def _(i):
+        out_copy(i).wait()
+
+
 def fused(length, vectors, reflectors, tau_diag, coupling):
     count, own, rows = reflectors.shape
     cols = vectors.shape[1]
     nb = own * length * CORES
     messages = length - 1
     hbm = pl.BlockSpec(memory_space=pl.ANY)
+    vmem = pl.BlockSpec(memory_space=pltpu.VMEM)
     dma = pltpu.SemaphoreType.DMA
-    return pl.pallas_call(
+    current, panel, updates = pl.pallas_call(
         functools.partial(kernel, length),
-        out_shape=pltpu.VMEM(vectors.shape, vectors.dtype),
+        out_shape=[
+            pltpu.VMEM(vectors.shape, vectors.dtype),
+            pltpu.VMEM((nb, rows), reflectors.dtype),
+            pltpu.VMEM((nb, 2 * cols), jnp.bfloat16),
+        ],
         in_specs=[hbm] * 4,
-        out_specs=pl.BlockSpec(memory_space=pltpu.VMEM),
+        out_specs=[vmem] * 3,
         scratch_shapes=[
-            pltpu.VMEM((count, nb, rows), reflectors.dtype),
+            pltpu.VMEM((count - 1, nb, rows), reflectors.dtype),
             pltpu.VMEM((rows, 2 * cols), jnp.bfloat16),
             pltpu.VMEM((nb, 2 * cols), jnp.float32),
             pltpu.VMEM((count, nb), jnp.float32),
             pltpu.VMEM((count, nb, nb), jnp.float32),
             pltpu.VMEM((nb, cols), jnp.float32),
-            pltpu.VMEM((nb, 2 * cols), jnp.bfloat16),
             pltpu.VMEM((count, nb, cols), jnp.float32),
             pltpu.VMEM((count, nb, cols), jnp.float32),
             dma((count,)),
@@ -308,9 +336,18 @@
             dma((count + 2,)),
         ],
         compiler_params=pltpu.CompilerParams(
-            collective_id=0, has_side_effects=True, vmem_limit_bytes=48 * 1024 * 1024
+            collective_id=0, has_side_effects=True, vmem_limit_bytes=40 * 1024 * 1024
         ),
     )(vectors, reflectors, tau_diag, coupling)
+    tiles = rows // min(1024, rows // 2)
+    return pl.pallas_call(
+        closing,
+        out_shape=jax.ShapeDtypeStruct(vectors.shape, vectors.dtype),
+        in_specs=[vmem] * 3,
+        out_specs=hbm,
+        scratch_shapes=[pltpu.VMEM(vectors.shape, jnp.float32), dma((tiles,))],
+        compiler_params=pltpu.CompilerParams(vmem_limit_bytes=16 * 1024 * 1024),
+    )(current, panel, updates)
 
 
 def on_device(two_rows, length, vectors, reflectors, tau_diag, coupling):

time: 183 us -> 181 us (0.989)
  local copies, waits for them, and re-layouts: 3.4 us -> 0 us
    unnamed x1 -> x0, local copies, waits for them, and re-layouts: 3.4 us -> none
    pallas_call x1 -> x2, Pallas kernels: 180 us -> 181 us  [the longest x1 174 us: fused(): pl.pallas_call(functools.partial(kernel, length), out_shape=[pltpu.VMEM(v...]
where the time goes in v4:
time: 181 us
  Pallas kernels  181 us (100%)
    pallas_call x1, Pallas kernels, fused(): pl.pallas_call(functools.partial(kernel, length), out_shape=[pltpu.VMEM(v...  174 us
    pallas_call x1, Pallas kernels, fused(): pl.pallas_call(closing, out_shape=jax.ShapeDtypeStruct(vectors.shape, vec...  6.73 us

profile of v4, /device:TPU:0, one launch (start us, length us, event | category | flops | bytes accessed | tf_op | source)
XLA Modules:
  0.0 180.7 jit_solution(12671680137482876011)
XLA Ops:
  0.0 174.0 %shard_map.46 = (f32[16384,128]{1,0:T(8,128)S(1)}, bf16[256,16384]{1,0:T(8,128)(2,1)S(1)}, bf16[256,256]{1,0:T(8,128)(2,1)S(1)}) custom-call(f32[16384,128]{1,0:T(8,128)} %z_hbm.1, bf16[4,16,16384]{2,1,0:T(8,128)(2,1)} %v_hbm.1, f32[4,256]{1,0:T(4,128)} %tau_hbm.1, f32[4,256,256]{2,1,0:T(8,128)} %coup_hbm.1), custom_call_target="tpu_custom_call" | custom-call | tf_op jit(solution)/shard_map/pallas_call | solution.py:310
  174.0 6.7 %shard_map.47 = f32[16384,128]{1,0:T(8,128)} custom-call(f32[16384,128]{1,0:T(8,128)S(1)} %get-tuple-element.8.z, bf16[256,16384]{1,0:T(8,128)(2,1)S(1)} %get-tuple-element.9.panel, bf16[256,256]{1,0:T(8,128)(2,1)S(1)} %get-tuple-element.10.yhl), custom_call_target="tpu_custom_call" | custom-call | tf_op jit(solution)/shard_map/pallas_call | solution.py:343
